TPU v7x, 32 devices: a whole 2x2x4 slice. The times are simulated.
32 devices in a mesh: grp: 2 (over y), seq: 4 (over z), head: 2 (over x), rep: 2 (over core).
Axes of the slice: x: 2, y: 2, z: 4, core: 2. Of those that a mesh axis runs over, the one named last changes fastest.
Arguments:
- x_proj: bfloat16 [4, 4, 4, 32, 8192], P(('grp', 'rep'), None, 'seq', None, 'head'), parts along dimension 0, may hold values from -6 to 6
- gate_proj: bfloat16 [4, 4, 4, 32, 8192], P(('grp', 'rep'), None, 'seq', None, 'head'), parts along dimension 0, may hold values from -6 to 6
- bc_proj: bfloat16 [4, 4, 4, 32, 256], P(('grp', 'rep'), None, 'seq'), parts along dimension 0, may hold values from -6 to 6
- dt_proj: bfloat16 [4, 4, 4, 32, 128], P(('grp', 'rep'), None, 'seq', None, 'head'), parts along dimension 0, may hold values from -5.5 to 7.5
- a_rate: float32 [128], P('head'), may hold values from 0.0001953125 to 0.05
- dt_bias: float32 [128], P('head'), may hold values from -1 to 1
- d_skip: float32 [128], P('head'), may hold values from 0.5 to 1.5
- conv_x_weight: float32 [4, 8192], P(None, 'head'), may hold values from -3 to 3
- conv_bc_weight: float32 [4, 256], replicated, may hold values from -3 to 3
- norm_gain: float32 [8192], P('head'), may hold values from 0.1 to 1.9
- out_weight: bfloat16 [8192, 2048], P(('seq', 'rep'), 'head'), may hold values from -0.0625 to 0.0625
- request_first_position: int32 [4], P(('grp', 'rep')), parts along dimension 0, may hold values from 0 to 255
- owner: int32 [4, 4], P(('grp', 'rep')), parts along dimension 0, may hold values from 0 to 3, each once within a row
Outputs:
- mixed: bfloat16 [4, 512, 2048], P(('grp', 'rep'), 'seq', 'head'), parts along dimension 0
- ssm_state: float32 [4, 4, 128, 2048], P(('grp', 'rep'), 'seq', 'head'), parts along dimension 0
- conv_x_state: bfloat16 [4, 4, 3, 2048], P(('grp', 'rep'), 'seq', None, 'head'), parts along dimension 0
- conv_bc_state: bfloat16 [4, 4, 3, 64], P(('grp', 'rep'), 'seq'), parts along dimension 0
There are 2 independent parts, one for each index of `grp`. A program takes and returns all parts, laid end to end along the dimension named above; an argument that names none is the same for every part. Nothing has to cross between parts.
Inputs may be any that keep to these rules, and one draw needn't show every extreme that they name: Each row of owner names every index of seq once.
All inputs are finite; a program needn't handle non-finite values.
Results may differ from a plain program's by a relative error of at most 0.007.
Values may be sent and summed in bfloat16 or wider, within the bound.
A program may use at most 128 MiB of HBM per device.

v0:
```python
import jax
import jax.numpy as jnp
from jax import lax
from jax.sharding import PartitionSpec as P

HEAD_DIM = 64
NSTATE = 128
KCONV = 4
SPAN = 128
INNER = 8192
highest = lax.Precision.HIGHEST
stability_constant = 1e-05


def passed_along(value, axis, by):
    devices = lax.axis_size(axis)
    pairs = [(i, i + by) for i in range(devices) if 0 <= i + by < devices]
    return lax.ppermute(value, axis, pairs)


def prefix(value, axis, combine, identity, reverse):
    devices, place = (lax.axis_size(axis), lax.axis_index(axis))
    everything = jax.tree.map(lambda part: lax.all_gather(part, axis), value)
    start = jax.tree.map(
        lambda part, zero: jnp.broadcast_to(jnp.asarray(zero, part.dtype), part.shape),
        value,
        identity,
    )

    def lap(k, before):
        at = devices - 1 - k if reverse else k
        reached = at > place if reverse else at < place
        new = combine(before, jax.tree.map(lambda part: part[at], everything))
        return jax.tree.map(lambda a, b: jnp.where(reached, a, b), new, before)

    return lax.fori_loop(0, devices, lap, start)


def broadcast(block, axis, source):
    block = jnp.where(lax.axis_index(axis) == source, block, jnp.zeros_like(block))
    return lax.psum(block, axis)


def span_terms(x_conv, b_rows, c_rows, step_size, log_decay):
    cum_decay = jnp.cumsum(log_decay, axis=1)
    scores = jnp.einsum("kqn,ktn->kqt", c_rows, b_rows, preferred_element_type=jnp.float32)
    cum_heads = jnp.swapaxes(cum_decay, 1, 2)
    step_heads = jnp.swapaxes(step_size, 1, 2)
    block_len = cum_decay.shape[1]
    causal = jnp.arange(block_len)[:, None] >= jnp.arange(block_len)[None, :]
    decay_gap = cum_heads[:, :, :, None] - cum_heads[:, :, None, :]
    seg_decay = jnp.exp(jnp.where(causal, decay_gap, -jnp.inf))
    weights = (scores[:, None] * seg_decay * step_heads[:, :, None, :]).astype(jnp.bfloat16)
    y_intra = jnp.einsum("khqt,kthp->kqhp", weights, x_conv, preferred_element_type=jnp.float32)
    remaining_length = jnp.exp(cum_decay[:, -1:, :] - cum_decay)
    scaled = ((remaining_length * step_size)[..., None] * x_conv.astype(jnp.float32)).astype(
        jnp.bfloat16
    )
    states = jnp.einsum("kthp,ktn->khpn", scaled, b_rows, preferred_element_type=jnp.float32)
    return (cum_decay, y_intra, states, jnp.exp(cum_decay[:, -1, :]))


def conv_silu(preceding_tokens, current, weight):
    extended = jnp.concatenate([preceding_tokens, current], axis=0)
    length = current.shape[0]
    accum = jnp.zeros(current.shape, jnp.float32)
    for offset in range(weight.shape[0]):
        accum = accum + weight[offset] * extended[offset : offset + length].astype(jnp.float32)
    return jax.nn.silu(accum)


def link(preceding_tokens, later):
    return (
        preceding_tokens[0] * later[0],
        later[0][:, None, None] * preceding_tokens[1] + later[1],
    )


def multiply(preceding_tokens, later):
    return preceding_tokens * later


def add_rows(source, piece):
    return jnp.dot(source, piece, preferred_element_type=jnp.float32)


def take_slab(values, slab_index, seq_count):
    grouped = values.reshape(values.shape[0], seq_count, -1)
    return lax.dynamic_index_in_dim(grouped, slab_index, axis=1, keepdims=False)


def local(
    x_proj,
    gate_proj,
    bc_proj,
    dt_proj,
    a_rate,
    dt_bias,
    d_skip,
    conv_x_weight,
    conv_bc_weight,
    norm_gain,
    out_weight,
    request_first_position,
    owner,
):
    x_all, z_all, bc_all, dt_all = (
        lax.all_to_all(x_proj, "seq", split_axis=1, concat_axis=2, tiled=True),
        lax.all_to_all(gate_proj, "seq", split_axis=1, concat_axis=2, tiled=True),
        lax.all_to_all(bc_proj, "seq", split_axis=1, concat_axis=2, tiled=True),
        lax.all_to_all(dt_proj, "seq", split_axis=1, concat_axis=2, tiled=True),
    )
    tokens_here = x_all.shape[2] * x_all.shape[3]
    x_local = x_all.reshape(tokens_here, x_all.shape[4])
    z_local = z_all.reshape(tokens_here, z_all.shape[4])
    bc_local = bc_all.reshape(tokens_here, bc_all.shape[4])
    dt_local = dt_all.reshape(tokens_here, dt_all.shape[4])
    heads = dt_local.shape[1]
    seq_index = lax.axis_index("seq")
    seq_count = lax.axis_size("seq")
    positions = seq_index * tokens_here + jnp.arange(tokens_here, dtype=jnp.int32)
    is_live = positions >= request_first_position[0]
    x_live = jnp.where(is_live[:, None], x_local, jnp.zeros_like(x_local))
    bc_live = jnp.where(is_live[:, None], bc_local, jnp.zeros_like(bc_local))
    rim_rows = KCONV - 1
    tail_x = x_live[tokens_here - rim_rows :]
    tail_bc = bc_live[tokens_here - rim_rows :]
    before_x, before_bc = passed_along((tail_x, tail_bc), "seq", 1)
    x_conv = conv_silu(before_x, x_live, conv_x_weight).astype(jnp.bfloat16)
    bc_conv = conv_silu(before_bc, bc_live, conv_bc_weight).astype(jnp.bfloat16)
    step_size = (
        jax.nn.softplus(dt_local.astype(jnp.float32) + dt_bias)
        * is_live.astype(jnp.float32)[:, None]
    )
    log_decay = -a_rate * step_size
    blocks = tokens_here // SPAN
    x_blocks = x_conv.reshape(blocks, SPAN, heads, HEAD_DIM)
    b_blocks = bc_conv[:, :NSTATE].reshape(blocks, SPAN, NSTATE)
    c_blocks = bc_conv[:, NSTATE:].reshape(blocks, SPAN, NSTATE)
    cum_decay, y_intra, states, decays = span_terms(
        x_blocks,
        b_blocks,
        c_blocks,
        step_size.reshape(blocks, SPAN, heads),
        log_decay.reshape(blocks, SPAN, heads),
    )

    def advance(carry, inputs):
        factor, contrib = inputs
        return (factor[:, None, None] * carry + contrib, carry)

    zero_state = jnp.zeros((heads, HEAD_DIM, NSTATE), jnp.float32)
    local_final, local_enter = lax.scan(advance, zero_state, (decays, states))
    dev_decay = jnp.prod(decays, axis=0)
    ones_heads = jnp.ones((heads,), jnp.float32)
    enter_decay, enter_state = prefix(
        (dev_decay, local_final), "seq", link, (ones_heads, zero_state), False
    )
    c_wide = c_blocks.astype(jnp.float32)
    before_block = jnp.concatenate([ones_heads[None], jnp.cumprod(decays, axis=0)[:-1]], axis=0)
    entering = local_enter + before_block[:, :, None, None] * enter_state[None]
    y_state = jnp.exp(cum_decay)[..., None] * jnp.einsum(
        "kqn,khpn->kqhp", c_wide, entering, precision=highest
    )
    y_total = y_intra + y_state + d_skip[:, None] * x_blocks.astype(jnp.float32)
    y_flat = y_total.reshape(tokens_here, heads * HEAD_DIM)
    gated = y_flat * jax.nn.silu(z_local.astype(jnp.float32))
    square_sums = lax.psum(jnp.sum(gated * gated, axis=1), "head")
    normed = (
        gated * lax.rsqrt(square_sums[:, None] / INNER + stability_constant) * norm_gain
    ).astype(jnp.bfloat16)
    last_index = seq_count - 1
    after_decay = prefix(dev_decay, "seq", multiply, ones_heads, True)
    final_state = lax.psum(after_decay[:, None, None] * local_final, "seq")
    keep_x, keep_bc = (broadcast(tail_x, "seq", last_index), broadcast(tail_bc, "seq", last_index))
    slab_index = jnp.sum(
        jnp.where(owner[0] == seq_index, jnp.arange(seq_count, dtype=jnp.int32), 0)
    )
    ssm_state = take_slab(final_state.reshape(heads, -1), slab_index, seq_count)[None, None]
    conv_x_state = take_slab(keep_x, slab_index, seq_count)[None, None]
    conv_bc_state = take_slab(keep_bc, slab_index, seq_count)[None, None]
    features = lax.all_gather(normed, "head", axis=1, tiled=True)
    out_cols = out_weight.shape[1]
    mixed_sum = add_rows(features, lax.all_gather(out_weight, ("seq", "rep"), axis=0, tiled=True))
    mixed = mixed_sum.astype(jnp.bfloat16).reshape(1, tokens_here, out_cols)
    return (mixed, ssm_state, conv_x_state, conv_bc_state)


def solution(mesh):
    return jax.shard_map(
        local,
        mesh=mesh,
        in_specs=(
            P(("grp", "rep"), None, "seq", None, "head"),
            P(("grp", "rep"), None, "seq", None, "head"),
            P(("grp", "rep"), None, "seq", None, None),
            P(("grp", "rep"), None, "seq", None, "head"),
            P("head"),
            P("head"),
            P("head"),
            P(None, "head"),
            P(),
            P("head"),
            P(("seq", "rep"), "head"),
            P(("grp", "rep")),
            P(("grp", "rep"), None),
        ),
        out_specs=(
            P(("grp", "rep"), "seq", "head"),
            P(("grp", "rep"), "seq", "head", None),
            P(("grp", "rep"), "seq", None, "head"),
            P(("grp", "rep"), "seq", None, None),
        ),
        check_vma=False,
    )
```

profile of v0, /device:TPU:0, one launch (start us, length us, event | category | flops | bytes accessed | tf_op | source)
XLA Modules:
  0.0 532.8 jit_solution(8478039113186121479)
XLA Ops:
  7.2 0.7 copy-done
  7.9 0.7 reshape.454
  8.6 6.3 %all-to-all-start.2 = ((bf16[4,2,1024]{2,1,0:T(2,128)(2,1)}), bf16[4,2,1024]{2,1,0:T(2,128)(2,1)S(1)}, u32[]{:S(2)}, u32[]{:S(2)}) async-start(bf16[4,2,1024]{2,1,0:T(2,128)(2,1)} %reshape.454), calls=%async_computation.2 | async-start | bytes 32768 | tf_op jit(solution)/shard_map/all_to_all | solution.py:111
  15.6 1.7 fusion.36
  17.3 1.4 fusion.37
  18.7 0.6 fusion.35
  19.3 0.7 neg.47
  20.0 0.6 all-to-all-done.2
  20.6 4.5 all-to-all-start.1
  25.2 0.7 broadcast_multiply_fusion.1
  25.9 0.2 reduce_window_sum.13
  26.1 0.7 bitcast_exponential_fusion
  26.9 0.2 mul.344
  27.1 1.9 copy.80
  29.0 11.5 %all-gather = f32[4,1,64]{2,1,0:T(1,128)S(1)} all-gather(f32[1,1,64]{2,1,0:T(1,128)S(1)} %get-tuple-element.290), channel_id=2, replica_groups=mesh['grp'=2,'seq'=4,'head'=2,'rep'=2] {'seq'}, dimensions={0}, use_global_device_ids=true | all-gather | bytes 1280 | tf_op jit(solution)/shard_map/all_gather | solution.py:23
  40.5 3.7 all-to-all-start
  44.2 0.6 exponential_multiply_fusion
  44.8 0.1 while.36
  45.0 0.9 bitcast_select_fusion.1
  46.0 0.6 broadcast_select_fusion.3
  46.6 3.8 collective-permute-start.1
  50.4 16.6 %all-to-all-done = bf16[1,4,1,32,4096]{4,3,2,0,1:T(8,128)(2,1)S(1)} async-done(((bf16[1,4,1,32,4096]{4,3,2,0,1:T(8,128)(2,1)}), bf16[1,4,1,32,4096]{4,3,2,0,1:T(8,128)(2,1)S(1)}, u32[]{:S(2)}, u32[]{:S(2)}) %all-to-all-start) | async-done | bytes 1048608 | tf_op jit(solution)/shard_map/all_to_all | solution.py:108
  67.0 0.2 bitcast_select_fusion
  67.3 1.3 collective-permute-start
  68.6 0.6 copy-done.16
  69.2 0.9 multiply_convert_fusion.4
  70.2 3.1 multiply_convert_fusion.2
  73.3 1.6 copy.81
  74.9 2.4 broadcast_multiply_fusion
  77.3 5.7 %all-to-all-start.3 = ((bf16[1,4,1,32,4096]{4,3,2,0,1:T(8,128)(2,1)}), bf16[1,4,1,32,4096]{4,3,2,0,1:T(8,128)(2,1)}, u32[]{:S(2)}, u32[]{:S(2)}) async-start(bf16[1,4,1,32,4096]{4,3,2,0,1:T(8,128)(2,1)} %bitcast.35), calls=%async_computation.3 | async-start | bytes 2097152 | tf_op jit(solution)/shard_map/all_to_all | solution.py:109
  83.5 48.3 %all-to-all-done.3 = bf16[1,4,1,32,4096]{4,3,2,0,1:T(8,128)(2,1)} async-done(((bf16[1,4,1,32,4096]{4,3,2,0,1:T(8,128)(2,1)}), bf16[1,4,1,32,4096]{4,3,2,0,1:T(8,128)(2,1)}, u32[]{:S(2)}, u32[]{:S(2)}) %all-to-all-start.3) | async-done | bytes 1048608 | tf_op jit(solution)/shard_map/all_to_all | solution.py:109
  131.8 2.7 bitcast_convert_fusion
  134.6 4.6 reshape.449
  139.2 4.8 copy.87
  144.0 1.3 copy.72
  145.3 1.7 copy.82
  147.0 3.0 reshape_reshape.3
  150.0 1.1 copy-done.4
  151.2 3.3 fusion.1
  154.4 87.4 %all-gather.10.cloned.1.call-done = f32[256,64,128]{2,1,0:T(8,128)} async-done(((f32[64,64,128]{2,1,0:T(8,128)}), f32[256,64,128]{2,1,0:T(8,128)}) %all-gather.10.cloned.1.call-update) | async-done | bytes 8388624 | tf_op jit(solution)/shard_map/all_gather | solution.py:23
  241.9 11.4 %while.35 = (s32[]{:T(128)}, f32[64,64,128]{2,1,0:T(8,128)S(1)}, s32[]{:T(128)}, f32[4,64]{1,0:T(4,128)}, f32[4,64,64,128]{3,2,1,0:T(8,128)}, /*index=5*/s32[]{:T(128)}, s32[]{:T(128)}) while((s32[]{:T(128)}, f32[64,64,128]{2,1,0:T(8,128)S(1)}, s32[]{:T(128)}, f32[4,64]{1,0:T(4,128)}, f32[4,64,64,128]{3,2,1,0:T(8,128)}, ...), condition=%wide.region_2.3_spmd.clone, body=%wide.region_1.2_spmd.clone.sunk | while | flops 2097156 | bytes 6292329 | solution.py:36
  241.9 0.7 dynamic-slice_bitcast_fusion.4
  242.6 2.1 fusion.44
  244.7 0.7 dynamic-slice_bitcast_fusion.4
  245.3 2.1 fusion.44
  247.4 0.7 dynamic-slice_bitcast_fusion.4
  248.1 2.3 fusion.44
  250.4 0.7 dynamic-slice_bitcast_fusion.4
  251.1 2.1 fusion.44
  253.2 5.9 %multiply_reduce_fusion = (f32[128]{0:T(128)S(1)}, f32[1,128,64,64]{1,3,2,0:T(8,128)}) fusion(f32[1,128,64,64]{1,3,2,0:T(8,128)} %copy.87, f32[1,128,64,64]{1,3,2,0:T(8,128)} %bitcast.133, f32[64]{0:T(128)S(1)} %copy-done.18, f32[64,64,128]{2,1,0:T(8,128)S(1)} %get-tuple-element.223, bf16[128,256]{1,0:T(8,128)(2,1)S(1)} %multiply_convert_fusion.4, ...), kind=kOutput, calls=%fused_computation.17 | convolution fusion | flops 811073408 | bytes 10552320 | tf_op jit(solution)/shard_map/kqn,khpn->kqhp/dot_general | solution.py:162
  259.1 3.1 copy.85
  262.2 4.9 psum.28
  267.1 3.3 fusion.14
  270.5 0.5 all-gather.8.cloned.1.call-update
  271.1 0.6 fusion.33
  273.7 18.3 %all-reduce = (bf16[3,4,1024]{2,0,1:T(4,128)(2,1)S(1)}, bf16[3,4,64]{2,0,1:T(4,128)(2,1)S(1)}) all-reduce(bf16[3,4,1024]{2,0,1:T(4,128)(2,1)S(1)} %bitcast.140, bf16[3,4,64]{2,0,1:T(4,128)(2,1)S(1)} %copy.89), channel_id=1, replica_groups=mesh['grp'=2,'seq'=4,'head'=2,'rep'=2] {'seq'}, use_global_device_ids=true, to_apply=%region_9.10 | all-reduce | flops 13056 | bytes 52224 | tf_op jit(solution)/shard_map/psum | solution.py:41
  292.1 0.6 dynamic-slice_bitcast_fusion.2
  292.6 0.6 dynamic-slice_bitcast_fusion.1
  293.2 37.3 %all-reduce.3.cloned.1.call-done = f32[64,4,2048]{2,1,0:T(4,128)} async-done(((f32[64,4,2048]{2,1,0:T(4,128)}), f32[64,4,2048]{2,1,0:T(4,128)}) %all-reduce.3.cloned.1.call-update) | async-done | bytes 2097168 | tf_op jit(solution)/shard_map/psum | solution.py:174
  330.5 2.1 constant_dynamic-slice_fusion
  332.7 1.0 copy.92
  333.6 30.6 %all-gather.6.cloned.1.call-done = bf16[128,8192]{1,0:T(8,128)(2,1)} async-done(((bf16[128,4096]{1,0:T(8,128)(2,1)}), bf16[128,8192]{1,0:T(8,128)(2,1)}) %all-gather.6.cloned.1.call-update) | async-done | bytes 2097168 | tf_op jit(solution)/shard_map/all_gather | solution.py:182
  364.2 152.6 %all-gather.8.cloned.1.call-done = bf16[8192,1024]{1,0:T(8,128)(2,1)} async-done(((bf16[1024,1024]{1,0:T(8,128)(2,1)}), bf16[8192,1024]{1,0:T(8,128)(2,1)}) %all-gather.8.cloned.1.call-update) | async-done | bytes 16777232 | tf_op jit(solution)/shard_map/all_gather | solution.py:184
  516.8 9.5 %fusion.16 = bf16[1,128,1024]{2,1,0:T(8,128)(2,1)} fusion(bf16[128,8192]{1,0:T(8,128)(2,1)} %all-gather.6.cloned.1.call-done, bf16[8192,1024]{1,0:T(8,128)(2,1)} %all-gather.8.cloned.1.call-done), kind=kOutput, calls=%fused_computation.31 | convolution fusion | flops 2147614720 | bytes 19136512 | tf_op jit(solution)/shard_map/dot_general | solution.py:84
  (67 shorter events, 1.2 us)
Async XLA Ops:
  7.2 0.8 copy-start
  8.6 12.0 %all-to-all-start.2 = ((bf16[4,2,1024]{2,1,0:T(2,128)(2,1)}), bf16[4,2,1024]{2,1,0:T(2,128)(2,1)S(1)}, u32[]{:S(2)}, u32[]{:S(2)}) async-start(bf16[4,2,1024]{2,1,0:T(2,128)(2,1)} %reshape.454), calls=%async_computation.2 | async-start | bytes 32768 | tf_op jit(solution)/shard_map/all_to_all | solution.py:111
  19.3 7.5 %copy-start.11 = (f32[128]{0:T(128)}, f32[128]{0:T(128)S(1)}, u32[]{:S(2)}) copy-start(f32[128]{0:T(128)S(1)} %get-tuple-element.282) | copy-start | bytes 1540
  20.6 19.9 %all-to-all-start.1 = ((bf16[1,4,1,32,256]{4,3,2,0,1:T(8,128)(2,1)}), bf16[1,4,1,32,256]{4,3,2,0,1:T(8,128)(2,1)S(1)}, u32[]{:S(2)}, u32[]{:S(2)}) async-start(bf16[1,4,1,32,256]{4,3,2,0,1:T(8,128)(2,1)} %bitcast.145), calls=%async_computation.1 | async-start | bytes 131072 | tf_op jit(solution)/shard_map/all_to_all | solution.py:110
  29.0 15.8 %copy-start.6 = (f32[64]{0:T(128)S(1)}, f32[64]{0:T(128)}, u32[]{:S(2)}) copy-start(f32[64]{0:T(128)} %custom-call.1) | copy-start | bytes 772
  29.0 16.0 %copy-start.15 = (pred[128]{0:T(512)(128)(4,1)S(1)}, pred[128]{0:T(512)(128)(4,1)}, u32[]{:S(2)}) copy-start(pred[128]{0:T(512)(128)(4,1)} %get-tuple-element.283) | copy-start | bytes 388
  40.5 4.5 copy-start.5
  40.5 29.6 %copy-start.3 = (f32[128,4096]{1,0:T(8,128)S(1)}, f32[128,4096]{1,0:T(8,128)}, u32[]{:S(2)}) copy-start(f32[128,4096]{1,0:T(8,128)} %copy.80) | copy-start | bytes 6291460
  40.5 26.5 %all-to-all-start = ((bf16[1,4,1,32,4096]{4,3,2,0,1:T(8,128)(2,1)}), bf16[1,4,1,32,4096]{4,3,2,0,1:T(8,128)(2,1)S(1)}, u32[]{:S(2)}, u32[]{:S(2)}) async-start(bf16[1,4,1,32,4096]{4,3,2,0,1:T(8,128)(2,1)} %bitcast.135), calls=%async_computation | async-start | bytes 2097152 | tf_op jit(solution)/shard_map/all_to_all | solution.py:108
  44.2 197.7 %all-gather.10.cloned.1.call-start = ((), (), s32[]{:S(2)}) async-start(), calls=%async_computation.7 | async-start | bytes 10485760 | tf_op jit(solution)/shard_map/all_gather | solution.py:23
  45.0 22.0 %copy-start.7 = (f32[64]{0:T(128)}, f32[64]{0:T(128)S(1)}, u32[]{:S(2)}) copy-start(f32[64]{0:T(128)S(1)} %get-tuple-element.224) | copy-start | bytes 772
  45.0 22.0 %copy-start.10 = (f32[4,64]{1,0:T(4,128)}, f32[4,64]{1,0:T(4,128)S(1)}, u32[]{:S(2)}) copy-start(f32[4,64]{1,0:T(4,128)S(1)} %get-tuple-element.430) | copy-start | bytes 3076
  46.6 22.0 %collective-permute-start.1 = (bf16[3,256]{1,0:T(4,128)(2,1)S(1)}, bf16[3,256]{1,0:T(4,128)(2,1)S(1)}, u32[]{:S(2)}, u32[]{:S(2)}) collective-permute-start(bf16[3,256]{1,0:T(4,128)(2,1)S(1)} %get-tuple-element.287), channel_id=1, source_target_pairs={{0,4},{4,8},{8,12},{1,5},{5,9},{9,13},{2,6},{6,10},{10,14},{3,7},{... | collective-permute-start | bytes 4616 | tf_op jit(solution)/shard_map/ppermute | solution.py:18
  67.3 2.9 collective-permute-start
  68.6 0.6 copy-start.16
  73.3 1.6 copy-start.8
  73.3 1.6 copy-start.17
  77.3 5.7 %copy-start.12 = (f32[128]{0:T(128)S(1)}, f32[128]{0:T(128)}, u32[]{:S(2)}) copy-start(f32[128]{0:T(128)} %copy-done.11) | copy-start | bytes 1540
  77.3 5.8 %copy-start.14 = (f32[64]{0:T(128)S(1)}, f32[64]{0:T(128)}, u32[]{:S(2)}) copy-start(f32[64]{0:T(128)} %param.22) | copy-start | bytes 772
  77.3 54.5 %all-to-all-start.3 = ((bf16[1,4,1,32,4096]{4,3,2,0,1:T(8,128)(2,1)}), bf16[1,4,1,32,4096]{4,3,2,0,1:T(8,128)(2,1)}, u32[]{:S(2)}, u32[]{:S(2)}) async-start(bf16[1,4,1,32,4096]{4,3,2,0,1:T(8,128)(2,1)} %bitcast.35), calls=%async_computation.3 | async-start | bytes 2097152 | tf_op jit(solution)/shard_map/all_to_all | solution.py:109
  83.0 247.5 %all-reduce.3.cloned.1.call-start = ((), (), s32[]{:S(2)}) async-start(), calls=%async_computation.6 | async-start | bytes 4194304 | tf_op jit(solution)/shard_map/psum | solution.py:174
  149.9 1.2 copy-start.4
  150.0 214.3 %all-gather.6.cloned.1.call-start = ((), (), s32[]{:S(2)}) async-start(), calls=%async_computation.4 | async-start | bytes 3145728 | tf_op jit(solution)/shard_map/all_gather | solution.py:182
  241.9 11.4 %copy-start.18 = (f32[64]{0:T(128)S(1)}, f32[64]{0:T(128)}, u32[]{:S(2)}) copy-start(f32[64]{0:T(128)} %param.23) | copy-start | bytes 772
  259.1 8.0 %copy-start.2 = (f32[1,4,1,32,4096]{4,3,1,2,0:T(8,128)S(1)}, f32[1,4,1,32,4096]{4,3,1,2,0:T(8,128)}, u32[]{:S(2)}) copy-start(f32[1,4,1,32,4096]{4,3,1,2,0:T(8,128)} %bitcast_convert_fusion) | copy-start | bytes 6291460
  259.1 8.0 %copy-start.9 = (f32[4096]{0:T(1024)S(1)}, f32[4096]{0:T(1024)}, u32[]{:S(2)}) copy-start(f32[4096]{0:T(1024)} %param.26) | copy-start | bytes 49156
  270.4 0.7 copy-start.19
  270.4 3.2 copy-start.13
  270.4 246.4 %all-gather.8.cloned.1.call-start = ((), (), s32[]{:S(2)}) async-start(), calls=%async_computation.5 | async-start | bytes 18874368 | tf_op jit(solution)/shard_map/all_gather | solution.py:184
  516.8 9.5 %copy-start.1 = (bf16[1,4,1,32,64]{4,3,2,1,0:T(8,128)(2,1)S(1)}, bf16[1,4,1,32,64]{4,3,2,1,0:T(8,128)(2,1)}, u32[]{:S(2)}) copy-start(bf16[1,4,1,32,64]{4,3,2,1,0:T(8,128)(2,1)} %param.20) | copy-start | bytes 49156
Sparse Core Ops, SparseCore 0:
  77.4 164.3 all-gather.9
  244.2 86.2 all-reduce.2
  332.1 32.1 all-gather.5
  365.7 151.0 all-gather.7
where the time goes:
time: 534 us; the launch traced here: 533 us
  waiting for transfers between devices  374 us (70%)
  local copies, waits for them, and re-layouts  36.1 us (7%)
  blocking collectives  34.7 us (6%)
  starting transfers between devices  25.4 us (5%)
  other arithmetic  24.6 us (5%)
  matrix products  21.1 us (4%)
  between operations  16.6 us (3%)
    all_gather x1, waiting for transfers between devices, local(): lax.all_gather(out_weight, ('seq', 'rep'), axis=0, tiled=True)  153 us
    all_gather x1, waiting for transfers between devices, prefix(): everything = jax.tree.map(lambda part: lax.all_gather(part, axis), value)  87.4 us
    all_to_all x1, waiting for transfers between devices, local(): lax.all_to_all(gate_proj, 'seq', split_axis=1, concat_axis=2, tiled=True)  48.3 us
    psum x1, waiting for transfers between devices, local(): final_state = lax.psum(after_decay[:, None, None] * local_final, 'seq')  37.3 us
    all_gather x1, waiting for transfers between devices, local(): features = lax.all_gather(normed, 'head', axis=1, tiled=True)  30.6 us
    psum x1, blocking collectives, broadcast(): return lax.psum(block, axis)  18.3 us
    all_to_all x1, waiting for transfers between devices, local(): lax.all_to_all(x_proj, 'seq', split_axis=1, concat_axis=2, tiled=True)  16.6 us
    all_gather x1, blocking collectives, prefix(): everything = jax.tree.map(lambda part: lax.all_gather(part, axis), value)  11.5 us
  transfers between devices with their start and end apart: 10, of which 8 were waited for; matrix products, arithmetic and copies ran while one was open for 12% of the time, Pallas kernels for 0%

commit v1 on v0

--- a/solution.py
+++ b/solution.py
@@ -179,7 +179,7 @@
     ssm_state = take_slab(final_state.reshape(heads, -1), slab_index, seq_count)[None, None]
     conv_x_state = take_slab(keep_x, slab_index, seq_count)[None, None]
     conv_bc_state = take_slab(keep_bc, slab_index, seq_count)[None, None]
-    features = lax.all_gather(normed, "head", axis=1, tiled=True)
+    features = jnp.concatenate(lax.all_gather(normed, "head"), axis=1)
     out_cols = out_weight.shape[1]
     mixed_sum = add_rows(features, lax.all_gather(out_weight, ("seq", "rep"), axis=0, tiled=True))
     mixed = mixed_sum.astype(jnp.bfloat16).reshape(1, tokens_here, out_cols)

time: 534 us -> 532 us (level)
  no operation moved by 1% of the time
where the time goes in v1:
time: 532 us; the launch traced here: 530 us
  waiting for transfers between devices  372 us (70%)
  local copies, waits for them, and re-layouts  37.8 us (7%)
  blocking collectives  34.7 us (7%)
  starting transfers between devices  25.4 us (5%)
  other arithmetic  23.4 us (4%)
  matrix products  20.5 us (4%)
  between operations  16.6 us (3%)
    all_gather x1, waiting for transfers between devices, local(): lax.all_gather(out_weight, ('seq', 'rep'), axis=0, tiled=True)  149 us
    all_gather x1, waiting for transfers between devices, prefix(): everything = jax.tree.map(lambda part: lax.all_gather(part, axis), value)  88.3 us
    all_to_all x1, waiting for transfers between devices, local(): lax.all_to_all(gate_proj, 'seq', split_axis=1, concat_axis=2, tiled=True)  48.2 us
    psum x1, waiting for transfers between devices, local(): final_state = lax.psum(after_decay[:, None, None] * local_final, 'seq')  37.4 us
    all_gather x1, waiting for transfers between devices, local(): features = jnp.concatenate(lax.all_gather(normed, 'head'), axis=1)  30.6 us
    psum x1, blocking collectives, broadcast(): return lax.psum(block, axis)  18.3 us
    all_to_all x1, waiting for transfers between devices, local(): lax.all_to_all(x_proj, 'seq', split_axis=1, concat_axis=2, tiled=True)  16.7 us
    all_gather x1, blocking collectives, prefix(): everything = jax.tree.map(lambda part: lax.all_gather(part, axis), value)  11.5 us
  transfers between devices with their start and end apart: 10, of which 8 were waited for; matrix products, arithmetic and copies ran while one was open for 12% of the time, Pallas kernels for 0%

profile of v1, /device:TPU:0, one launch (start us, length us, event | category | flops | bytes accessed | tf_op | source)
XLA Modules:
  0.0 530.5 jit_solution(8030545253947052130)
XLA Ops:
  7.2 0.7 copy-done
  7.9 0.7 reshape.544
  8.6 6.3 %all-to-all-start.2 = ((bf16[4,2,1024]{2,1,0:T(2,128)(2,1)}), bf16[4,2,1024]{2,1,0:T(2,128)(2,1)S(1)}, u32[]{:S(2)}, u32[]{:S(2)}) async-start(bf16[4,2,1024]{2,1,0:T(2,128)(2,1)} %reshape.544), calls=%async_computation.2 | async-start | bytes 32768 | tf_op jit(solution)/shard_map/all_to_all | solution.py:111
  15.6 1.7 fusion.29
  17.3 1.4 fusion.30
  18.7 0.6 fusion.28
  19.3 0.7 neg.54
  20.0 0.6 all-to-all-done.2
  20.6 4.5 all-to-all-start.1
  25.2 0.7 broadcast_multiply_fusion.1
  25.9 0.2 reduce_window_sum.13
  26.1 0.7 bitcast_exponential_fusion
  26.9 0.2 mul.372
  27.1 1.9 copy.81
  29.0 11.5 %all-gather = f32[4,1,64]{2,1,0:T(1,128)S(1)} all-gather(f32[1,1,64]{2,1,0:T(1,128)S(1)} %get-tuple-element.290), channel_id=2, replica_groups=mesh['grp'=2,'seq'=4,'head'=2,'rep'=2] {'seq'}, dimensions={0}, use_global_device_ids=true | all-gather | bytes 1280 | tf_op jit(solution)/shard_map/all_gather | solution.py:23
  40.5 3.7 all-to-all-start
  44.2 0.6 exponential_multiply_fusion
  44.9 0.9 bitcast_select_fusion.1
  45.9 0.6 broadcast_select_fusion.3
  46.5 3.8 collective-permute-start.1
  50.3 16.7 %all-to-all-done = bf16[1,4,1,32,4096]{4,3,2,0,1:T(8,128)(2,1)S(1)} async-done(((bf16[1,4,1,32,4096]{4,3,2,0,1:T(8,128)(2,1)}), bf16[1,4,1,32,4096]{4,3,2,0,1:T(8,128)(2,1)S(1)}, u32[]{:S(2)}, u32[]{:S(2)}) %all-to-all-start) | async-done | bytes 1048608 | tf_op jit(solution)/shard_map/all_to_all | solution.py:108
  67.0 0.2 bitcast_select_fusion
  67.2 1.3 collective-permute-start
  68.5 0.6 copy-done.17
  69.1 0.9 multiply_convert_fusion.5
  70.1 3.1 multiply_convert_fusion.3
  73.2 0.7 copy.82
  73.9 2.4 broadcast_multiply_fusion
  76.3 5.7 %all-to-all-start.3 = ((bf16[1,4,1,32,4096]{4,3,2,0,1:T(8,128)(2,1)}), bf16[1,4,1,32,4096]{4,3,2,0,1:T(8,128)(2,1)S(1)}, u32[]{:S(2)}, u32[]{:S(2)}) async-start(bf16[1,4,1,32,4096]{4,3,2,0,1:T(8,128)(2,1)} %bitcast.35), calls=%async_computation.3 | async-start | bytes 2097152 | tf_op jit(solution)/shard_map/all_to_all | solution.py:109
  82.5 48.2 %all-to-all-done.3 = bf16[1,4,1,32,4096]{4,3,2,0,1:T(8,128)(2,1)S(1)} async-done(((bf16[1,4,1,32,4096]{4,3,2,0,1:T(8,128)(2,1)}), bf16[1,4,1,32,4096]{4,3,2,0,1:T(8,128)(2,1)S(1)}, u32[]{:S(2)}, u32[]{:S(2)}) %all-to-all-start.3) | async-done | bytes 1048608 | tf_op jit(solution)/shard_map/all_to_all | solution.py:109
  130.7 3.3 reshape.539
  134.0 4.8 copy.87
  138.8 1.6 convert_element_type.168
  140.4 2.4 copy.73
  142.7 1.7 copy.83
  144.4 2.9 reshape_reshape.3
  147.4 1.1 copy-done.5
  148.6 3.3 fusion.1
  151.8 88.3 %all-gather.10.cloned.1.call-done = f32[256,64,128]{2,1,0:T(8,128)} async-done(((f32[64,64,128]{2,1,0:T(8,128)}), f32[256,64,128]{2,1,0:T(8,128)}) %all-gather.10.cloned.1.call-update) | async-done | bytes 8388624 | tf_op jit(solution)/shard_map/all_gather | solution.py:23
  240.1 11.4 %while.35 = (s32[]{:T(128)}, f32[64,64,128]{2,1,0:T(8,128)S(1)}, s32[]{:T(128)}, f32[4,64]{1,0:T(4,128)}, f32[4,64,64,128]{3,2,1,0:T(8,128)}, /*index=5*/s32[]{:T(128)}, s32[]{:T(128)}) while((s32[]{:T(128)}, f32[64,64,128]{2,1,0:T(8,128)S(1)}, s32[]{:T(128)}, f32[4,64]{1,0:T(4,128)}, f32[4,64,64,128]{3,2,1,0:T(8,128)}, ...), condition=%wide.region_2.3_spmd.clone, body=%wide.region_1.2_spmd.clone.sunk | while | flops 2097156 | bytes 6292329 | solution.py:36
  240.1 0.7 dynamic-slice_bitcast_fusion.4
  240.8 2.1 fusion.37
  242.9 0.7 dynamic-slice_bitcast_fusion.4
  243.6 2.1 fusion.37
  245.7 0.7 dynamic-slice_bitcast_fusion.4
  246.4 2.3 fusion.37
  248.7 0.7 dynamic-slice_bitcast_fusion.4
  249.4 2.1 fusion.37
  251.5 5.8 %multiply_reduce_fusion = (f32[128]{0:T(128)S(1)}, f32[1,128,64,64]{1,3,2,0:T(8,128)}) fusion(f32[1,128,64,64]{1,3,2,0:T(8,128)} %copy.87, f32[1,128,64,64]{1,3,2,0:T(8,128)} %bitcast.118, f32[64]{0:T(128)S(1)} %copy-done.19, f32[64,64,128]{2,1,0:T(8,128)S(1)} %get-tuple-element.223, bf16[128,256]{1,0:T(8,128)(2,1)S(1)} %multiply_convert_fusion.5, ...), kind=kOutput, calls=%fused_computation.10 | convolution fusion | flops 811073408 | bytes 10552320 | tf_op jit(solution)/shard_map/kqn,khpn->kqhp/dot_general | solution.py:162
  257.3 3.1 copy.85
  260.4 4.9 psum.28
  265.3 3.3 multiply_convert_fusion.2
  268.7 0.5 all-gather.8.cloned.1.call-update
  269.2 0.6 fusion.26
  271.9 18.3 %all-reduce = (bf16[3,4,1024]{2,0,1:T(4,128)(2,1)S(1)}, bf16[3,4,64]{2,0,1:T(4,128)(2,1)S(1)}) all-reduce(bf16[3,4,1024]{2,0,1:T(4,128)(2,1)S(1)} %bitcast.125, bf16[3,4,64]{2,0,1:T(4,128)(2,1)S(1)} %copy.90), channel_id=1, replica_groups=mesh['grp'=2,'seq'=4,'head'=2,'rep'=2] {'seq'}, use_global_device_ids=true, to_apply=%region_9.10 | all-reduce | flops 13056 | bytes 52224 | tf_op jit(solution)/shard_map/psum | solution.py:41
  290.2 0.6 dynamic-slice_bitcast_fusion.2
  290.8 0.6 dynamic-slice_bitcast_fusion.1
  291.4 37.4 %all-reduce.3.cloned.1.call-done = f32[64,4,2048]{2,1,0:T(4,128)} async-done(((f32[64,4,2048]{2,1,0:T(4,128)}), f32[64,4,2048]{2,1,0:T(4,128)}) %all-reduce.3.cloned.1.call-update) | async-done | bytes 2097168 | tf_op jit(solution)/shard_map/psum | solution.py:174
  328.8 2.1 constant_dynamic-slice_fusion
  331.0 1.0 copy.93
  331.9 30.6 %all-gather.6.cloned.1.call-done = bf16[2,128,4096]{2,1,0:T(8,128)(2,1)} async-done(((bf16[1,128,4096]{2,1,0:T(8,128)(2,1)}), bf16[2,128,4096]{2,1,0:T(8,128)(2,1)}) %all-gather.6.cloned.1.call-update) | async-done | bytes 2097168 | tf_op jit(solution)/shard_map/all_gather | solution.py:182
  362.5 3.1 copy.88
  365.7 149.4 %all-gather.8.cloned.1.call-done = bf16[8192,1024]{1,0:T(8,128)(2,1)} async-done(((bf16[1024,1024]{1,0:T(8,128)(2,1)}), bf16[8192,1024]{1,0:T(8,128)(2,1)}) %all-gather.8.cloned.1.call-update) | async-done | bytes 16777232 | tf_op jit(solution)/shard_map/all_gather | solution.py:184
  515.1 8.8 %fusion.9 = bf16[1,128,1024]{2,1,0:T(8,128)(2,1)} fusion(bf16[128,8192]{0,1:T(8,128)(2,1)S(1)} %bitcast.114, bf16[8192,1024]{1,0:T(8,128)(2,1)} %all-gather.8.cloned.1.call-done), kind=kOutput, calls=%fused_computation.23 | convolution fusion | flops 2147614720 | bytes 19136512 | tf_op jit(solution)/shard_map/dot_general | solution.py:84
  (70 shorter events, 1.4 us)
Async XLA Ops:
  7.2 0.8 copy-start
  8.6 12.0 %all-to-all-start.2 = ((bf16[4,2,1024]{2,1,0:T(2,128)(2,1)}), bf16[4,2,1024]{2,1,0:T(2,128)(2,1)S(1)}, u32[]{:S(2)}, u32[]{:S(2)}) async-start(bf16[4,2,1024]{2,1,0:T(2,128)(2,1)} %reshape.544), calls=%async_computation.2 | async-start | bytes 32768 | tf_op jit(solution)/shard_map/all_to_all | solution.py:111
  19.3 7.5 %copy-start.12 = (f32[128]{0:T(128)}, f32[128]{0:T(128)S(1)}, u32[]{:S(2)}) copy-start(f32[128]{0:T(128)S(1)} %get-tuple-element.282) | copy-start | bytes 1540
  20.6 19.9 %all-to-all-start.1 = ((bf16[1,4,1,32,256]{4,3,2,0,1:T(8,128)(2,1)}), bf16[1,4,1,32,256]{4,3,2,0,1:T(8,128)(2,1)S(1)}, u32[]{:S(2)}, u32[]{:S(2)}) async-start(bf16[1,4,1,32,256]{4,3,2,0,1:T(8,128)(2,1)} %bitcast.130), calls=%async_computation.1 | async-start | bytes 131072 | tf_op jit(solution)/shard_map/all_to_all | solution.py:110
  29.0 15.8 %copy-start.7 = (f32[64]{0:T(128)S(1)}, f32[64]{0:T(128)}, u32[]{:S(2)}) copy-start(f32[64]{0:T(128)} %custom-call.1) | copy-start | bytes 772
  29.0 16.0 %copy-start.16 = (pred[128]{0:T(512)(128)(4,1)S(1)}, pred[128]{0:T(512)(128)(4,1)}, u32[]{:S(2)}) copy-start(pred[128]{0:T(512)(128)(4,1)} %get-tuple-element.283) | copy-start | bytes 388
  40.5 4.4 copy-start.6
  40.5 29.6 %copy-start.4 = (f32[128,4096]{1,0:T(8,128)S(1)}, f32[128,4096]{1,0:T(8,128)}, u32[]{:S(2)}) copy-start(f32[128,4096]{1,0:T(8,128)} %copy.81) | copy-start | bytes 6291460
  40.5 26.5 %all-to-all-start = ((bf16[1,4,1,32,4096]{4,3,2,0,1:T(8,128)(2,1)}), bf16[1,4,1,32,4096]{4,3,2,0,1:T(8,128)(2,1)S(1)}, u32[]{:S(2)}, u32[]{:S(2)}) async-start(bf16[1,4,1,32,4096]{4,3,2,0,1:T(8,128)(2,1)} %bitcast.120), calls=%async_computation | async-start | bytes 2097152 | tf_op jit(solution)/shard_map/all_to_all | solution.py:108
  44.1 196.0 %all-gather.10.cloned.1.call-start = ((), (), s32[]{:S(2)}) async-start(), calls=%async_computation.7 | async-start | bytes 10485760 | tf_op jit(solution)/shard_map/all_gather | solution.py:23
  44.9 22.1 %copy-start.8 = (f32[64]{0:T(128)}, f32[64]{0:T(128)S(1)}, u32[]{:S(2)}) copy-start(f32[64]{0:T(128)S(1)} %get-tuple-element.224) | copy-start | bytes 772
  44.9 22.1 %copy-start.11 = (f32[4,64]{1,0:T(4,128)}, f32[4,64]{1,0:T(4,128)S(1)}, u32[]{:S(2)}) copy-start(f32[4,64]{1,0:T(4,128)S(1)} %get-tuple-element.431) | copy-start | bytes 3076
  46.5 22.1 %collective-permute-start.1 = (bf16[3,256]{1,0:T(4,128)(2,1)S(1)}, bf16[3,256]{1,0:T(4,128)(2,1)S(1)}, u32[]{:S(2)}, u32[]{:S(2)}) collective-permute-start(bf16[3,256]{1,0:T(4,128)(2,1)S(1)} %get-tuple-element.287), channel_id=1, source_target_pairs={{0,4},{4,8},{8,12},{1,5},{5,9},{9,13},{2,6},{6,10},{10,14},{3,7},{... | collective-permute-start | bytes 4616 | tf_op jit(solution)/shard_map/ppermute | solution.py:18
  67.2 2.9 collective-permute-start
  68.5 0.6 copy-start.17
  73.2 0.7 copy-start.9
  73.2 0.7 copy-start.18
  76.3 5.7 %copy-start.13 = (f32[128]{0:T(128)S(1)}, f32[128]{0:T(128)}, u32[]{:S(2)}) copy-start(f32[128]{0:T(128)} %copy-done.12) | copy-start | bytes 1540
  76.3 5.8 %copy-start.15 = (f32[64]{0:T(128)S(1)}, f32[64]{0:T(128)}, u32[]{:S(2)}) copy-start(f32[64]{0:T(128)} %param.22) | copy-start | bytes 772
  76.3 54.4 %all-to-all-start.3 = ((bf16[1,4,1,32,4096]{4,3,2,0,1:T(8,128)(2,1)}), bf16[1,4,1,32,4096]{4,3,2,0,1:T(8,128)(2,1)S(1)}, u32[]{:S(2)}, u32[]{:S(2)}) async-start(bf16[1,4,1,32,4096]{4,3,2,0,1:T(8,128)(2,1)} %bitcast.35), calls=%async_computation.3 | async-start | bytes 2097152 | tf_op jit(solution)/shard_map/all_to_all | solution.py:109
  82.0 246.8 %all-reduce.3.cloned.1.call-start = ((), (), s32[]{:S(2)}) async-start(), calls=%async_computation.6 | async-start | bytes 4194304 | tf_op jit(solution)/shard_map/psum | solution.py:174
  140.4 2.4 copy-start.2
  147.3 1.2 copy-start.5
  147.4 215.2 %all-gather.6.cloned.1.call-start = ((), (), s32[]{:S(2)}) async-start(), calls=%async_computation.4 | async-start | bytes 3145728 | tf_op jit(solution)/shard_map/all_gather | solution.py:182
  240.1 11.4 %copy-start.19 = (f32[64]{0:T(128)S(1)}, f32[64]{0:T(128)}, u32[]{:S(2)}) copy-start(f32[64]{0:T(128)} %param.23) | copy-start | bytes 772
  257.3 8.0 %copy-start.3 = (f32[1,4,1,32,4096]{4,3,2,0,1:T(8,128)S(1)}, f32[1,4,1,32,4096]{4,3,2,0,1:T(8,128)}, u32[]{:S(2)}) copy-start(f32[1,4,1,32,4096]{4,3,2,0,1:T(8,128)} %convert_element_type.168) | copy-start | bytes 6291460
  257.3 8.0 %copy-start.10 = (f32[4096]{0:T(1024)S(1)}, f32[4096]{0:T(1024)}, u32[]{:S(2)}) copy-start(f32[4096]{0:T(1024)} %param.26) | copy-start | bytes 49156
  268.6 0.7 copy-start.20
  268.6 3.2 copy-start.14
  268.6 246.5 %all-gather.8.cloned.1.call-start = ((), (), s32[]{:S(2)}) async-start(), calls=%async_computation.5 | async-start | bytes 18874368 | tf_op jit(solution)/shard_map/all_gather | solution.py:184
  515.1 8.8 %copy-start.1 = (bf16[1,4,1,32,64]{4,3,2,1,0:T(8,128)(2,1)S(1)}, bf16[1,4,1,32,64]{4,3,2,1,0:T(8,128)(2,1)}, u32[]{:S(2)}) copy-start(bf16[1,4,1,32,64]{4,3,2,1,0:T(8,128)(2,1)} %param.20) | copy-start | bytes 49156
Sparse Core Ops, SparseCore 0:
  76.4 163.6 all-gather.9
  242.5 86.2 all-reduce.2
  330.4 32.1 all-gather.5
  364.0 151.0 all-gather.7
